TPU v7x, 32 devices: a whole 2x2x4 slice. The times are simulated.
32 devices in a mesh: py: 2 (over x), px: 4 (over y, core), pz: 4 (over z).
Axes of the slice: x: 2, y: 2, z: 4, core: 2. Of those that a mesh axis runs over, the one named last changes fastest.
Arguments:
- initial_density: float32 [8, 256, 384, 128], P('py', 'px', 'pz'), may hold values from 0.2 to 1.8
- inverse_limit: float32 [8, 256, 384, 128], P('py', 'px', 'pz'), may hold values from 0.5 to 2
Outputs:
- temperature_end: float32 [8, 256, 384, 128], P('py', 'px', 'pz')
All inputs are finite; a program needn't handle non-finite values.
Results may differ from a plain program's by a relative error of at most 0.00002.
Values sent between devices are 32-bit elements; how exact they have to be, the bound alone decides.
A program may use at most 384 MiB of HBM per device.

v0:
```python
import jax
import jax.numpy as jnp
from jax import lax
from jax.sharding import PartitionSpec as P

STEPS = 3


def padded(cells, sides, width):
    for axis, dim in sides:
        count = lax.axis_size(axis)
        ends = count - 1
        head = lax.slice_in_dim(cells, 0, width, axis=dim)
        tail = lax.slice_in_dim(cells, cells.shape[dim] - width, cells.shape[dim], axis=dim)
        cells = jnp.concatenate(
            [
                lax.ppermute(tail, axis, [(i, (i + 1) % count) for i in range(ends)]),
                cells,
                lax.ppermute(head, axis, [((i + 1) % count, i) for i in range(ends)]),
            ],
            axis=dim,
        )
    return cells


def inner_cells(values, dims):
    for dim in dims:
        values = lax.slice_in_dim(values, 1, values.shape[dim] - 1, axis=dim)
    return values


def boundary_cells(values, dim, start, dims):
    remaining_parts = [other for other in dims if other != dim]
    values = inner_cells(values, remaining_parts)
    return lax.slice_in_dim(values, start, start + values.shape[dim] - 2, axis=dim)


def advance_population(haloed_population, inverse_limit):
    middle = inner_cells(haloed_population, (0, 1, 2))
    lower = [boundary_cells(haloed_population, dim, 0, (0, 1, 2)) for dim in (0, 1, 2)]
    upper = [boundary_cells(haloed_population, dim, 2, (0, 1, 2)) for dim in (0, 1, 2)]
    spread = lower[0] + upper[0] + lower[1] + upper[1] + lower[2] + upper[2] - 6.0 * middle
    return middle + 0.1 * spread + 0.2 * middle * (1.0 - middle * inverse_limit)


def local(initial_density, inverse_limit):
    for step in range(STEPS):
        haloed_population = padded(initial_density, (("py", 0), ("px", 1), ("pz", 2)), 1)
        initial_density = advance_population(haloed_population, inverse_limit)
    return initial_density


def solution(mesh):
    in_specs = (P("py", "px", "pz", None), P("py", "px", "pz", None))
    out_specs = P("py", "px", "pz", None)
    return jax.shard_map(local, mesh=mesh, in_specs=in_specs, out_specs=out_specs, check_vma=False)
```

profile of v0, /device:TPU:0, one launch (start us, length us, event | category | flops | bytes accessed | tf_op | source)
XLA Modules:
  0.0 438.0 jit_solution(17570152833986694887)
XLA Ops:
  0.0 5.0 %fusion.30 = (f32[1,64,96,128]{3,2,1,0:T(8,128)}, f32[1,64,96,128]{3,2,1,0:T(8,128)S(1)}) fusion(f32[4,64,96,128]{3,2,1,0:T(8,128)} %param.2), kind=kLoop, calls=%fused_computation.98 | loop fusion | bytes 12582912 | tf_op jit(solution)/shard_map/slice | solution.py:13
  5.0 5.1 %collective-permute-start = (f32[1,64,96,128]{3,2,1,0:T(8,128)S(1)}, f32[1,64,96,128]{3,2,1,0:T(8,128)S(1)}, u32[]{:S(2)}, u32[]{:S(2)}) collective-permute-start(f32[1,64,96,128]{3,2,1,0:T(8,128)S(1)} %get-tuple-element.22), channel_id=1, source_target_pairs={{0,16},{1,17},{2,18},{3,19},{4,20},{5,21},{6,22},{7,23},{8,24},{9,... | collective-permute-start | bytes 9437192 | tf_op jit(solution)/shard_map/ppermute | solution.py:17
  11.3 65.8 %collective-permute-done = f32[1,64,96,128]{3,2,1,0:T(8,128)S(1)} collective-permute-done((f32[1,64,96,128]{3,2,1,0:T(8,128)S(1)}, f32[1,64,96,128]{3,2,1,0:T(8,128)S(1)}, u32[]{:S(2)}, u32[]{:S(2)}) %collective-permute-start) | collective-permute-done | bytes 3145760 | tf_op jit(solution)/shard_map/ppermute | solution.py:17
  77.2 1.8 constant_dynamic-update-slice_fusion.2
  79.0 10.3 %constant_dynamic-update-slice_fusion.1 = f32[6,64,96,128]{3,2,1,0:T(8,128)} fusion(f32[6,64,96,128]{3,2,1,0:T(8,128)} %constant_dynamic-update-slice_fusion.2, f32[4,64,96,128]{3,2,1,0:T(8,128)} %param.2), kind=kLoop, calls=%fused_computation.93 | loop fusion | bytes 25165824
  89.3 2.0 constant_dynamic-update-slice_fusion
  92.5 1.3 collective-permute-start.2
  95.2 3.9 collective-permute-done.3
  99.1 2.3 pad_maximum_fusion.64
  101.4 1.3 collective-permute-start.5
  102.8 4.6 %collective-permute-start.4 = (f32[6,66,1,128]{3,1,2,0:T(8,128)S(1)}, f32[6,66,1,128]{3,1,2,0:T(8,128)S(1)}, u32[]{:S(2)}, u32[]{:S(2)}) collective-permute-start(f32[6,66,1,128]{3,1,2,0:T(8,128)S(1)} %copy.16), channel_id=1, source_target_pairs={{0,1},{1,2},{2,3},{4,5},{5,6},{6,7},{8,9},{9,10},{10,11},{12,13},{... | collective-permute-start | bytes 608264 | tf_op jit(solution)/shard_map/ppermute | solution.py:17
  107.3 1.9 collective-permute-done.5
  111.6 42.6 %fusion.22 = f32[4,64,96,128]{3,2,1,0:T(8,128)} fusion(f32[4,64,96,128]{3,2,1,0:T(8,128)} %param.2, f32[6,66,1,128]{3,2,1,0:T(1,128)} %copy.19, f32[6,1,96,128]{3,2,1,0:T(8,128)} %copy-done.5, f32[6,64,96,128]{3,2,1,0:T(8,128)} %constant_dynamic-update-slice_fusion, f32[6,1,96,128]{3,2,1,0:T(8,128)S(1)} %collective-permute-done.2, ...), kind=kLoop, calls=%fused_computation.59 | loop fusion | flops 75497472 | bytes 63909888 | tf_op jit(solution)/shard_map/add | solution.py:43
  154.2 3.4 fusion.29
  157.7 4.9 %collective-permute-start.6 = (f32[1,64,96,128]{3,2,1,0:T(8,128)S(1)}, f32[1,64,96,128]{3,2,1,0:T(8,128)S(1)}, u32[]{:S(2)}, u32[]{:S(2)}) collective-permute-start(f32[1,64,96,128]{3,2,1,0:T(8,128)S(1)} %get-tuple-element.19), channel_id=1, source_target_pairs={{0,16},{1,17},{2,18},{3,19},{4,20},{5,21},{6,22},{7,23},{8,24},{9,... | collective-permute-start | bytes 9437192 | tf_op jit(solution)/shard_map/ppermute | solution.py:17
  163.9 64.0 %collective-permute-done.6 = f32[1,64,96,128]{3,2,1,0:T(8,128)S(1)} collective-permute-done((f32[1,64,96,128]{3,2,1,0:T(8,128)S(1)}, f32[1,64,96,128]{3,2,1,0:T(8,128)S(1)}, u32[]{:S(2)}, u32[]{:S(2)}) %collective-permute-start.6) | collective-permute-done | bytes 3145760 | tf_op jit(solution)/shard_map/ppermute | solution.py:17
  227.9 4.9 %collective-permute-done.7 = f32[1,64,96,128]{3,2,1,0:T(8,128)S(1)} collective-permute-done((f32[1,64,96,128]{3,2,1,0:T(8,128)S(1)}, f32[1,64,96,128]{3,2,1,0:T(8,128)S(1)}, u32[]{:S(2)}, u32[]{:S(2)}) %collective-permute-start.7) | collective-permute-done | bytes 3145760 | tf_op jit(solution)/shard_map/ppermute | solution.py:19
  232.8 4.4 %collective-permute-start.8 = (f32[6,1,96,128]{3,2,1,0:T(8,128)S(1)}, f32[6,1,96,128]{3,2,1,0:T(8,128)S(1)}, u32[]{:S(2)}, u32[]{:S(2)}) collective-permute-start(f32[6,1,96,128]{3,2,1,0:T(8,128)S(1)} %get-tuple-element.13), channel_id=1, source_target_pairs={{0,4},{4,8},{8,12},{1,5},{5,9},{9,13},{2,6},{6,10},{10,14},{3,7},{... | collective-permute-start | bytes 884744 | tf_op jit(solution)/shard_map/ppermute | solution.py:17
  238.5 2.2 collective-permute-done.9
  242.8 5.2 %collective-permute-start.10 = (f32[6,66,1,128]{3,1,2,0:T(8,128)S(1)}, f32[6,66,1,128]{3,1,2,0:T(8,128)S(1)}, u32[]{:S(2)}, u32[]{:S(2)}) collective-permute-start(f32[6,66,1,128]{3,1,2,0:T(8,128)S(1)} %copy.20), channel_id=1, source_target_pairs={{0,1},{1,2},{2,3},{4,5},{5,6},{6,7},{8,9},{9,10},{10,11},{12,13},{... | collective-permute-start | bytes 608264 | tf_op jit(solution)/shard_map/ppermute | solution.py:17
  248.0 1.8 collective-permute-done.11
  252.1 45.2 %fusion.13 = f32[4,64,96,128]{3,2,1,0:T(8,128)} fusion(f32[4,64,96,128]{3,2,1,0:T(8,128)} %fusion.22, f32[6,66,1,128]{3,2,1,0:T(1,128)} %copy.23, f32[6,1,96,128]{3,2,1,0:T(8,128)} %copy-done.6, f32[6,1,96,128]{3,2,1,0:T(8,128)S(1)} %collective-permute-done.8, f32[1,64,96,128]{3,2,1,0:T(8,128)} %copy-done.2, ...), kind=kLoop, calls=%fused_computation.32 | loop fusion | flops 100663296 | bytes 45035520 | tf_op jit(solution)/shard_map/add | solution.py:43
  297.3 3.4 fusion.28
  300.7 2.3 collective-permute-start.12
  303.1 1.3 collective-permute-start.13
  304.4 64.2 %collective-permute-done.12 = f32[1,64,96,128]{3,2,1,0:T(8,128)S(1)} collective-permute-done((f32[1,64,96,128]{3,2,1,0:T(8,128)S(1)}, f32[1,64,96,128]{3,2,1,0:T(8,128)S(1)}, u32[]{:S(2)}, u32[]{:S(2)}) %collective-permute-start.12) | collective-permute-done | bytes 3145760 | tf_op jit(solution)/shard_map/ppermute | solution.py:17
  368.6 4.9 %collective-permute-done.13 = f32[1,64,96,128]{3,2,1,0:T(8,128)S(1)} collective-permute-done((f32[1,64,96,128]{3,2,1,0:T(8,128)S(1)}, f32[1,64,96,128]{3,2,1,0:T(8,128)S(1)}, u32[]{:S(2)}, u32[]{:S(2)}) %collective-permute-start.13) | collective-permute-done | bytes 3145760 | tf_op jit(solution)/shard_map/ppermute | solution.py:19
  373.5 4.2 collective-permute-start.14
  379.1 2.2 collective-permute-done.15
  383.3 5.0 %collective-permute-start.16 = (f32[6,66,1,128]{3,1,2,0:T(8,128)S(1)}, f32[6,66,1,128]{3,1,2,0:T(8,128)S(1)}, u32[]{:S(2)}, u32[]{:S(2)}) collective-permute-start(f32[6,66,1,128]{3,1,2,0:T(8,128)S(1)} %copy.24), channel_id=1, source_target_pairs={{0,1},{1,2},{2,3},{4,5},{5,6},{6,7},{8,9},{9,10},{10,11},{12,13},{... | collective-permute-start | bytes 608264 | tf_op jit(solution)/shard_map/ppermute | solution.py:17
  388.3 1.9 collective-permute-done.17
  392.6 45.2 %fusion.4 = f32[4,64,96,128]{3,2,1,0:T(8,128)} fusion(f32[4,64,96,128]{3,2,1,0:T(8,128)} %fusion.13, f32[6,66,1,128]{3,2,1,0:T(1,128)} %copy.27, f32[6,1,96,128]{3,2,1,0:T(8,128)} %copy-done.7, f32[6,1,96,128]{3,2,1,0:T(8,128)S(1)} %collective-permute-done.14, f32[1,64,96,128]{3,2,1,0:T(8,128)} %copy-done.3, ...), kind=kLoop, calls=%fused_computation.5 | loop fusion | flops 100663296 | bytes 45035520 | tf_op jit(solution)/shard_map/add | solution.py:43
  (47 shorter events, 19.0 us)
Async XLA Ops:
  5.0 72.2 %collective-permute-start = (f32[1,64,96,128]{3,2,1,0:T(8,128)S(1)}, f32[1,64,96,128]{3,2,1,0:T(8,128)S(1)}, u32[]{:S(2)}, u32[]{:S(2)}) collective-permute-start(f32[1,64,96,128]{3,2,1,0:T(8,128)S(1)} %get-tuple-element.22), channel_id=1, source_target_pairs={{0,16},{1,17},{2,18},{3,19},{4,20},{5,21},{6,22},{7,23},{8,24},{9,... | collective-permute-start | bytes 9437192 | tf_op jit(solution)/shard_map/ppermute | solution.py:17
  10.0 79.3 %collective-permute-start.1 = (f32[1,64,96,128]{3,2,1,0:T(8,128)}, f32[1,64,96,128]{3,2,1,0:T(8,128)S(1)}, u32[]{:S(2)}, u32[]{:S(2)}) collective-permute-start(f32[1,64,96,128]{3,2,1,0:T(8,128)} %get-tuple-element.21), channel_id=1, source_target_pairs={{16,0},{17,1},{18,2},{19,3},{20,4},{21,5},{22,6},{23,7},{24,8},{25... | collective-permute-start | bytes 9437192 | tf_op jit(solution)/shard_map/ppermute | solution.py:19
  89.3 12.1 %copy-start.4 = (f32[1,64,96,128]{3,2,1,0:T(8,128)}, f32[1,64,96,128]{3,2,1,0:T(8,128)S(1)}, u32[]{:S(2)}) copy-start(f32[1,64,96,128]{3,2,1,0:T(8,128)S(1)} %collective-permute-done.1) | copy-start | bytes 9437188
  92.5 2.6 collective-permute-start.2
  93.8 5.2 %collective-permute-start.3 = (f32[6,1,96,128]{3,2,1,0:T(8,128)S(1)}, f32[6,1,96,128]{3,2,1,0:T(8,128)S(1)}, u32[]{:S(2)}, u32[]{:S(2)}) collective-permute-start(f32[6,1,96,128]{3,2,1,0:T(8,128)S(1)} %get-tuple-element.16), channel_id=1, source_target_pairs={{4,0},{8,4},{12,8},{5,1},{9,5},{13,9},{6,2},{10,6},{14,10},{7,3},{... | collective-permute-start | bytes 884744 | tf_op jit(solution)/shard_map/ppermute | solution.py:19
  99.1 2.3 copy-start.5
  101.4 7.8 %collective-permute-start.5 = (f32[6,66,1,128]{3,1,2,0:T(8,128)S(1)}, f32[6,66,1,128]{3,1,2,0:T(8,128)S(1)}, u32[]{:S(2)}, u32[]{:S(2)}) collective-permute-start(f32[6,66,1,128]{3,1,2,0:T(8,128)S(1)} %copy.18), channel_id=1, source_target_pairs={{1,0},{2,1},{3,2},{5,4},{6,5},{7,6},{9,8},{10,9},{11,10},{13,12},{... | collective-permute-start | bytes 608264 | tf_op jit(solution)/shard_map/ppermute | solution.py:19
  102.8 8.0 %collective-permute-start.4 = (f32[6,66,1,128]{3,1,2,0:T(8,128)S(1)}, f32[6,66,1,128]{3,1,2,0:T(8,128)S(1)}, u32[]{:S(2)}, u32[]{:S(2)}) collective-permute-start(f32[6,66,1,128]{3,1,2,0:T(8,128)S(1)} %copy.16), channel_id=1, source_target_pairs={{0,1},{1,2},{2,3},{4,5},{5,6},{6,7},{8,9},{9,10},{10,11},{12,13},{... | collective-permute-start | bytes 608264 | tf_op jit(solution)/shard_map/ppermute | solution.py:17
  154.2 78.5 %copy-start = (f32[4,64,96,128]{3,2,1,0:T(8,128)S(1)}, f32[4,64,96,128]{3,2,1,0:T(8,128)}, u32[]{:S(2)}) copy-start(f32[4,64,96,128]{3,2,1,0:T(8,128)} %fusion.22) | copy-start | bytes 37748740
  157.7 70.2 %collective-permute-start.6 = (f32[1,64,96,128]{3,2,1,0:T(8,128)S(1)}, f32[1,64,96,128]{3,2,1,0:T(8,128)S(1)}, u32[]{:S(2)}, u32[]{:S(2)}) collective-permute-start(f32[1,64,96,128]{3,2,1,0:T(8,128)S(1)} %get-tuple-element.19), channel_id=1, source_target_pairs={{0,16},{1,17},{2,18},{3,19},{4,20},{5,21},{6,22},{7,23},{8,24},{9,... | collective-permute-start | bytes 9437192 | tf_op jit(solution)/shard_map/ppermute | solution.py:17
  162.6 70.2 %collective-permute-start.7 = (f32[1,64,96,128]{3,2,1,0:T(8,128)S(1)}, f32[1,64,96,128]{3,2,1,0:T(8,128)S(1)}, u32[]{:S(2)}, u32[]{:S(2)}) collective-permute-start(f32[1,64,96,128]{3,2,1,0:T(8,128)S(1)} %get-tuple-element.20), channel_id=1, source_target_pairs={{16,0},{17,1},{18,2},{19,3},{20,4},{21,5},{22,6},{23,7},{24,8},{25... | collective-permute-start | bytes 9437192 | tf_op jit(solution)/shard_map/ppermute | solution.py:19
  232.8 8.2 %copy-start.2 = (f32[1,64,96,128]{3,2,1,0:T(8,128)}, f32[1,64,96,128]{3,2,1,0:T(8,128)S(1)}, u32[]{:S(2)}) copy-start(f32[1,64,96,128]{3,2,1,0:T(8,128)S(1)} %collective-permute-done.7) | copy-start | bytes 9437188
  232.8 5.7 %collective-permute-start.8 = (f32[6,1,96,128]{3,2,1,0:T(8,128)S(1)}, f32[6,1,96,128]{3,2,1,0:T(8,128)S(1)}, u32[]{:S(2)}, u32[]{:S(2)}) collective-permute-start(f32[6,1,96,128]{3,2,1,0:T(8,128)S(1)} %get-tuple-element.13), channel_id=1, source_target_pairs={{0,4},{4,8},{8,12},{1,5},{5,9},{9,13},{2,6},{6,10},{10,14},{3,7},{... | collective-permute-start | bytes 884744 | tf_op jit(solution)/shard_map/ppermute | solution.py:17
  237.2 3.5 collective-permute-start.9
  240.7 0.7 copy-start.6
  241.4 8.3 %collective-permute-start.11 = (f32[6,66,1,128]{3,1,2,0:T(8,128)S(1)}, f32[6,66,1,128]{3,1,2,0:T(8,128)S(1)}, u32[]{:S(2)}, u32[]{:S(2)}) collective-permute-start(f32[6,66,1,128]{3,1,2,0:T(8,128)S(1)} %copy.22), channel_id=1, source_target_pairs={{1,0},{2,1},{3,2},{5,4},{6,5},{7,6},{9,8},{10,9},{11,10},{13,12},{... | collective-permute-start | bytes 608264 | tf_op jit(solution)/shard_map/ppermute | solution.py:19
  242.8 8.5 %collective-permute-start.10 = (f32[6,66,1,128]{3,1,2,0:T(8,128)S(1)}, f32[6,66,1,128]{3,1,2,0:T(8,128)S(1)}, u32[]{:S(2)}, u32[]{:S(2)}) collective-permute-start(f32[6,66,1,128]{3,1,2,0:T(8,128)S(1)} %copy.20), channel_id=1, source_target_pairs={{0,1},{1,2},{2,3},{4,5},{5,6},{6,7},{8,9},{9,10},{10,11},{12,13},{... | collective-permute-start | bytes 608264 | tf_op jit(solution)/shard_map/ppermute | solution.py:17
  297.3 76.2 %copy-start.1 = (f32[4,64,96,128]{3,2,1,0:T(8,128)S(1)}, f32[4,64,96,128]{3,2,1,0:T(8,128)}, u32[]{:S(2)}) copy-start(f32[4,64,96,128]{3,2,1,0:T(8,128)} %fusion.13) | copy-start | bytes 37748740
  300.7 67.9 %collective-permute-start.12 = (f32[1,64,96,128]{3,2,1,0:T(8,128)S(1)}, f32[1,64,96,128]{3,2,1,0:T(8,128)S(1)}, u32[]{:S(2)}, u32[]{:S(2)}) collective-permute-start(f32[1,64,96,128]{3,2,1,0:T(8,128)S(1)} %get-tuple-element.17), channel_id=1, source_target_pairs={{0,16},{1,17},{2,18},{3,19},{4,20},{5,21},{6,22},{7,23},{8,24},{9,... | collective-permute-start | bytes 9437192 | tf_op jit(solution)/shard_map/ppermute | solution.py:17
  303.1 70.4 %collective-permute-start.13 = (f32[1,64,96,128]{3,2,1,0:T(8,128)S(1)}, f32[1,64,96,128]{3,2,1,0:T(8,128)S(1)}, u32[]{:S(2)}, u32[]{:S(2)}) collective-permute-start(f32[1,64,96,128]{3,2,1,0:T(8,128)S(1)} %get-tuple-element.18), channel_id=1, source_target_pairs={{16,0},{17,1},{18,2},{19,3},{20,4},{21,5},{22,6},{23,7},{24,8},{25... | collective-permute-start | bytes 9437192 | tf_op jit(solution)/shard_map/ppermute | solution.py:19
  373.5 8.0 %copy-start.3 = (f32[1,64,96,128]{3,2,1,0:T(8,128)}, f32[1,64,96,128]{3,2,1,0:T(8,128)S(1)}, u32[]{:S(2)}) copy-start(f32[1,64,96,128]{3,2,1,0:T(8,128)S(1)} %collective-permute-done.13) | copy-start | bytes 9437188
  373.5 5.5 %collective-permute-start.14 = (f32[6,1,96,128]{3,2,1,0:T(8,128)S(1)}, f32[6,1,96,128]{3,2,1,0:T(8,128)S(1)}, u32[]{:S(2)}, u32[]{:S(2)}) collective-permute-start(f32[6,1,96,128]{3,2,1,0:T(8,128)S(1)} %get-tuple-element.11), channel_id=1, source_target_pairs={{0,4},{4,8},{8,12},{1,5},{5,9},{9,13},{2,6},{6,10},{10,14},{3,7},{... | collective-permute-start | bytes 884744 | tf_op jit(solution)/shard_map/ppermute | solution.py:17
  377.7 3.5 collective-permute-start.15
  381.2 0.7 copy-start.7
  381.9 8.3 %collective-permute-start.17 = (f32[6,66,1,128]{3,1,2,0:T(8,128)S(1)}, f32[6,66,1,128]{3,1,2,0:T(8,128)S(1)}, u32[]{:S(2)}, u32[]{:S(2)}) collective-permute-start(f32[6,66,1,128]{3,1,2,0:T(8,128)S(1)} %copy.26), channel_id=1, source_target_pairs={{1,0},{2,1},{3,2},{5,4},{6,5},{7,6},{9,8},{10,9},{11,10},{13,12},{... | collective-permute-start | bytes 608264 | tf_op jit(solution)/shard_map/ppermute | solution.py:19
  383.3 8.5 %collective-permute-start.16 = (f32[6,66,1,128]{3,1,2,0:T(8,128)S(1)}, f32[6,66,1,128]{3,1,2,0:T(8,128)S(1)}, u32[]{:S(2)}, u32[]{:S(2)}) collective-permute-start(f32[6,66,1,128]{3,1,2,0:T(8,128)S(1)} %copy.24), channel_id=1, source_target_pairs={{0,1},{1,2},{2,3},{4,5},{5,6},{6,7},{8,9},{9,10},{10,11},{12,13},{... | collective-permute-start | bytes 608264 | tf_op jit(solution)/shard_map/ppermute | solution.py:17
where the time goes:
time: 442 us; the launch traced here: 438 us
  waiting for transfers between devices  219 us (50%)
  other arithmetic  136 us (31%)
  starting transfers between devices  48.6 us (11%)
  local copies, waits for them, and re-layouts  33.5 us (8%)
    ppermute x9, waiting for transfers between devices, padded(): lax.ppermute(tail, axis, [(i, (i + 1) % count) for i in range(ends)])  196 us
    add x3, other arithmetic, advance_population(): return middle + 0.1 * spread + 0.2 * middle * (1.0 - middle * inverse_limit)  133 us
    ppermute x9, starting transfers between devices, padded(): lax.ppermute(tail, axis, [(i, (i + 1) % count) for i in range(ends)])  37 us
    ppermute x9, waiting for transfers between devices, padded(): lax.ppermute(head, axis, [((i + 1) % count, i) for i in range(ends)])  23.6 us
    unnamed x18, local copies, waits for them, and re-layouts  13 us
    ppermute x9, starting transfers between devices, padded(): lax.ppermute(head, axis, [((i + 1) % count, i) for i in range(ends)])  11.6 us
  transfers between devices with their start and end apart: 18, of which 14 were waited for; matrix products, arithmetic and copies ran while one was open for 3% of the time, Pallas kernels for 0%

commit v1 on v0

v1 whole, which is shorter than its diff:
```python
import functools

import jax
import jax.numpy as jnp
from jax import lax
from jax.experimental import pallas as pl
from jax.experimental.pallas import tpu as pltpu
from jax.sharding import PartitionSpec as P

STEPS = 3
MESH = pl.DeviceIdType.MESH


def chunk_rows(rows):
    for parts in (8, 4, 2):
        if rows % parts == 0 and rows // parts >= 2:
            return rows // parts
    return rows


def kernel(sizes, x_ref, il_ref, out_ref, a_ref, il_v, hy, hx, hz, zs,
           load_sem, y_send, y_recv, x_send, x_recv, z_send, z_recv):
    ny, nx, nz = sizes
    planes, rows, depth, lanes = a_ref.shape
    size = chunk_rows(rows)
    chunks = rows // size
    axes = (("py", ny), ("px", nx), ("pz", nz))
    me = {axis: lax.axis_index(axis) for axis, _ in axes}
    has = {axis: (me[axis] > 0, me[axis] < n - 1) for axis, n in axes}

    def other(axis, side):
        return {axis: me[axis] + (2 * side - 1)}

    barrier = pltpu.get_barrier_semaphore()
    for axis, _ in axes:
        for side in (0, 1):
            @pl.when(has[axis][side])
            def _():
                pl.semaphore_signal(barrier, inc=1, device_id=other(axis, side), device_id_type=MESH)
    pl.semaphore_wait(barrier, sum(flag.astype(jnp.int32) for pair in has.values() for flag in pair))

    level = (a_ref, out_ref, a_ref, out_ref)

    def y_copy(step, side, c):
        span = pl.ds(c * size, size)
        source = x_ref if step == 0 else level[step]
        return pltpu.make_async_remote_copy(
            src_ref=source.at[(planes - 1) * side, span],
            dst_ref=hy.at[1 - side, step, span],
            send_sem=y_send.at[side, step, c],
            recv_sem=y_recv.at[1 - side, step, c],
            device_id=other("py", side), device_id_type=MESH)

    def y_landed(step, side, c):
        span = pl.ds(c * size, size)
        return pltpu.make_async_remote_copy(
            src_ref=x_ref.at[0, span],
            dst_ref=hy.at[side, step, span],
            send_sem=y_send.at[side, step, c],
            recv_sem=y_recv.at[side, step, c],
            device_id=other("py", side), device_id_type=MESH)

    def x_copy(step, side):
        return pltpu.make_async_remote_copy(
            src_ref=level[step].at[:, (rows - 1) * side],
            dst_ref=hx.at[1 - side, step],
            send_sem=x_send.at[side, step],
            recv_sem=x_recv.at[1 - side, step],
            device_id=other("px", side), device_id_type=MESH)

    def x_landed(step, side):
        return pltpu.make_async_remote_copy(
            src_ref=hx.at[side, step],
            dst_ref=hx.at[side, step],
            send_sem=x_send.at[side, step],
            recv_sem=x_recv.at[side, step],
            device_id=other("px", side), device_id_type=MESH)

    def z_copy(step, side):
        return pltpu.make_async_remote_copy(
            src_ref=zs.at[side, step],
            dst_ref=hz.at[1 - side, step],
            send_sem=z_send.at[side, step],
            recv_sem=z_recv.at[1 - side, step],
            device_id=other("pz", side), device_id_type=MESH)

    def z_landed(step, side):
        return pltpu.make_async_remote_copy(
            src_ref=hz.at[side, step],
            dst_ref=hz.at[side, step],
            send_sem=z_send.at[side, step],
            recv_sem=z_recv.at[side, step],
            device_id=other("pz", side), device_id_type=MESH)

    def start_y(step, c):
        for side in (0, 1):
            @pl.when(has["py"][side])
            def _():
                y_copy(step, side, c).start()

    def on_faces(make, axis, act):
        for side in (0, 1):
            @pl.when(has[axis][side])
            def _():
                act(make(side))

    @pl.loop(0, chunks)
    def _(c):
        start_y(0, c)

    loads = [
        pltpu.make_async_copy(x_ref.at[y], a_ref.at[y], load_sem.at[0, y]) for y in range(planes)
    ] + [
        pltpu.make_async_copy(il_ref.at[y], il_v.at[y], load_sem.at[1, y]) for y in range(planes)
    ]
    for load in loads:
        load.start()

    for side in (0, 1):
        @pl.when(jnp.logical_not(has["py"][side]))
        def _():
            for step in range(STEPS):
                @pl.loop(0, rows)
                def _(r):
                    hy[side, step, r] = jnp.zeros((depth, lanes), jnp.float32)

        @pl.when(jnp.logical_not(has["px"][side]))
        def _():
            for step in range(STEPS):
                for y in range(planes):
                    hx[side, step, y] = jnp.zeros((depth, lanes), jnp.float32)

        @pl.when(jnp.logical_not(has["pz"][side]))
        def _():
            for step in range(STEPS):
                for y in range(planes):
                    hz[side, step, y] = jnp.zeros((rows, lanes), jnp.float32)

    for load in loads:
        load.wait()

    @pl.loop(0, rows)
    def _(r):
        for y in range(planes):
            zs[0, 0, y, pl.ds(r, 1), :] = a_ref[y, r, 0:1, :]
            zs[1, 0, y, pl.ds(r, 1), :] = a_ref[y, r, depth - 1:depth, :]

    on_faces(functools.partial(x_copy, 0), "px", lambda copy: copy.start())
    on_faces(functools.partial(z_copy, 0), "pz", lambda copy: copy.start())

    place = lax.broadcasted_iota(jnp.int32, (depth, lanes), 0)

    def advance(step, r, below, above):
        old, new = level[step], level[step + 1]
        for y in range(planes):
            middle = old[y, r]
            first = hz[0, step, y, pl.ds(r, 1), :]
            last = hz[1, step, y, pl.ds(r, 1), :]
            total = below(y) + above(y)
            total += hy[0, step, r] if y == 0 else old[y - 1, r]
            total += hy[1, step, r] if y == planes - 1 else old[y + 1, r]
            total += jnp.where(place == 0, first, pltpu.roll(middle, 1, 0))
            total += jnp.where(place == depth - 1, last, pltpu.roll(middle, depth - 1, 0))
            value = 0.1 * total + middle * (0.6 - 0.2 * (middle * il_v[y, r]))
            new[y, r] = value
            if step < STEPS - 1:
                zs[0, step + 1, y, pl.ds(r, 1), :] = value[0:1]
                zs[1, step + 1, y, pl.ds(r, 1), :] = value[depth - 1:depth]

    for step in range(STEPS):
        old = level[step]

        on_faces(functools.partial(x_landed, step), "px", lambda copy: copy.wait_recv())
        on_faces(functools.partial(z_landed, step), "pz", lambda copy: copy.wait_recv())
        if step > 0:
            on_faces(functools.partial(x_copy, step - 1), "px", lambda copy: copy.wait_send())

        def arrive(c, step=step):
            for side in (0, 1):
                @pl.when(has["py"][side])
                def _():
                    y_landed(step, side, c).wait_recv()
                    if step > 0:
                        y_copy(step - 1, side, c).wait_send()

        def span(low, high, step=step, old=old):
            @pl.loop(low, high)
            def _(r):
                advance(step, r, lambda y: old[y, r - 1], lambda y: old[y, r + 1])

        arrive(0)
        advance(step, 0, lambda y: hx[0, step, y], lambda y: old[y, 1])
        span(1, size)

        @pl.loop(1, chunks - 1)
        def _(c):
            arrive(c)
            span(c * size, c * size + size)
            if step < STEPS - 1:
                start_y(step + 1, c - 1)

        arrive(chunks - 1)
        span(rows - size, rows - 1)
        advance(step, rows - 1, lambda y: old[y, rows - 2], lambda y: hx[1, step, y])
        if step < STEPS - 1:
            start_y(step + 1, chunks - 2)
            on_faces(functools.partial(x_copy, step + 1), "px", lambda copy: copy.start())
            on_faces(functools.partial(z_copy, step + 1), "pz", lambda copy: copy.start())
            start_y(step + 1, chunks - 1)

    on_faces(functools.partial(x_copy, STEPS - 1), "px", lambda copy: copy.wait_send())
    for step in range(STEPS):
        on_faces(functools.partial(z_copy, step), "pz", lambda copy: copy.wait_send())

    @pl.loop(0, chunks)
    def _(c):
        on_faces(lambda side: y_copy(STEPS - 1, side, c), "py", lambda copy: copy.wait_send())


def local(sizes, initial_density, inverse_limit):
    planes, rows, depth, lanes = initial_density.shape
    chunks = rows // chunk_rows(rows)
    dma = pltpu.SemaphoreType.DMA
    return pl.pallas_call(
        functools.partial(kernel, sizes),
        out_shape=pltpu.VMEM(initial_density.shape, jnp.float32),
        in_specs=[pl.BlockSpec(memory_space=pltpu.HBM)] * 2,
        out_specs=pl.BlockSpec(memory_space=pltpu.VMEM),
        scratch_shapes=[
            pltpu.VMEM((planes, rows, depth, lanes), jnp.float32),
            pltpu.VMEM((planes, rows, depth, lanes), jnp.float32),
            pltpu.VMEM((2, STEPS, rows, depth, lanes), jnp.float32),
            pltpu.VMEM((2, STEPS, planes, depth, lanes), jnp.float32),
            pltpu.VMEM((2, STEPS, planes, rows, lanes), jnp.float32),
            pltpu.VMEM((2, STEPS, planes, rows, lanes), jnp.float32),
            dma((2, planes)),
            dma((2, STEPS, chunks)), dma((2, STEPS, chunks)),
            dma((2, STEPS)), dma((2, STEPS)), dma((2, STEPS)), dma((2, STEPS)),
        ],
        compiler_params=pltpu.CompilerParams(
            collective_id=0, has_side_effects=True, vmem_limit_bytes=50 * 2**20),
        name="populate",
    )(initial_density, inverse_limit)


def solution(mesh):
    sizes = tuple(mesh.shape[axis] for axis in ("py", "px", "pz"))
    spec = P("py", "px", "pz", None)
    return jax.shard_map(functools.partial(local, sizes), mesh=mesh, in_specs=(spec, spec), out_specs=spec, check_vma=False)
```

time: 442 us -> 215 us (0.49)
  waiting for transfers between devices: 219 us -> 0 us
  Pallas kernels: 0 us -> 210 us
  other arithmetic: 136 us -> 0 us
  starting transfers between devices: 48.6 us -> 0 us
  local copies, waits for them, and re-layouts: 33.5 us -> 4.78 us
    ppermute x18 -> x0, waiting for transfers between devices: 219 us -> none  [the longest x9 196 us: padded(): lax.ppermute(tail, axis, [(i, (i + 1) % count) for i in range(ends)])]
    pallas_call x0 -> x1, Pallas kernels: none -> 210 us  [local(): pl.pallas_call(functools.partial(kernel, sizes), out_shape=pltpu.VMEM(ini...]
    add x3 -> x0, other arithmetic: 133 us -> none  [advance_population(): return middle + 0.1 * spread + 0.2 * middle * (1.0 - middle * inverse_limit)]
    ppermute x18 -> x0, starting transfers between devices: 48.6 us -> none  [the longest x9 37 us: padded(): lax.ppermute(tail, axis, [(i, (i + 1) % count) for i in range(ends)])]
    slice x10 -> x0, local copies, waits for them, and re-layouts: 13.1 us -> none  [the longest x6 8.14 us: padded(): lax.slice_in_dim(cells, cells.shape[dim] - width, cells.shape[dim], axis=...]
    unnamed x18 -> x1, local copies, waits for them, and re-layouts: 13 us -> 4.78 us
    ppermute x6 -> x0, local copies, waits for them, and re-layouts: 5.41 us -> none  [the longest x3 2.72 us: padded(): lax.ppermute(head, axis, [((i + 1) % count, i) for i in range(ends)])]
  transfers between devices with their start and end apart: 18 -> 0, of which waited for: 14 -> 0; matrix products, arithmetic and copies ran while one was open for 3% -> 0% of each run, Pallas kernels for 0% -> 0%
where the time goes in v1:
time: 215 us
  Pallas kernels  210 us (98%)
  local copies, waits for them, and re-layouts  4.78 us (2%)
    pallas_call x1, Pallas kernels, local(): pl.pallas_call(functools.partial(kernel, sizes), out_shape=pltpu.VMEM(ini...  210 us
    unnamed x1, local copies, waits for them, and re-layouts  4.78 us

profile of v1, /device:TPU:0, one launch (start us, length us, event | category | flops | bytes accessed | tf_op | source)
XLA Modules:
  0.0 214.7 jit_solution(8773417570112371339)
XLA Ops:
  0.0 209.9 %populate.1 = f32[4,64,96,128]{3,2,1,0:T(8,128)S(1)} custom-call(f32[4,64,96,128]{3,2,1,0:T(8,128)} %x_ref.1, f32[4,64,96,128]{3,2,1,0:T(8,128)} %il_ref.1), custom_call_target="tpu_custom_call" | custom-call | tf_op jit(solution)/shard_map/populate/pallas_call | solution.py:224
  209.9 4.8 %copy.4 = f32[4,64,96,128]{3,2,1,0:T(8,128)} copy(f32[4,64,96,128]{3,2,1,0:T(8,128)S(1)} %populate.1) | data formatting | bytes 25165824

commit v2 on v1

--- a/solution.py
+++ b/solution.py
@@ -8,11 +8,12 @@
 from jax.sharding import PartitionSpec as P
 
 STEPS = 3
+PARTS = 4
 MESH = pl.DeviceIdType.MESH
 
 
 def chunk_rows(rows):
-    for parts in (8, 4, 2):
+    for parts in (16, 8, 4, 2):
         if rows % parts == 0 and rows // parts >= 2:
             return rows // parts
     return rows
@@ -150,9 +151,9 @@
 
     place = lax.broadcasted_iota(jnp.int32, (depth, lanes), 0)
 
-    def advance(step, r, below, above):
+    def advance(step, r, below, above, ys=tuple(range(planes))):
         old, new = level[step], level[step + 1]
-        for y in range(planes):
+        for y in ys:
             middle = old[y, r]
             first = hz[0, step, y, pl.ds(r, 1), :]
             last = hz[1, step, y, pl.ds(r, 1), :]
@@ -167,61 +168,115 @@
                 zs[0, step + 1, y, pl.ds(r, 1), :] = value[0:1]
                 zs[1, step + 1, y, pl.ds(r, 1), :] = value[depth - 1:depth]
 
+    def span(step, low, high, ys):
+        old = level[step]
+
+        @pl.loop(low, high)
+        def _(r):
+            advance(step, r, lambda y: old[y, r - 1], lambda y: old[y, r + 1], ys)
+
+    def head_rows(step, high, ys):
+        old = level[step]
+        advance(step, 0, lambda y: hx[0, step, y], lambda y: old[y, 1], ys)
+        span(step, 1, high, ys)
+
+    def tail_rows(step, low, ys):
+        old = level[step]
+        span(step, low, rows - 1, ys)
+        advance(step, rows - 1, lambda y: old[y, rows - 2], lambda y: hx[1, step, y], ys)
+
+    def arrive(step, side, c):
+        y_landed(step, side, c).wait_recv()
+        if step > 0:
+            y_copy(step - 1, side, c).wait_send()
+
+    every = tuple(range(planes))
     for step in range(STEPS):
-        old = level[step]
-
         on_faces(functools.partial(x_landed, step), "px", lambda copy: copy.wait_recv())
         on_faces(functools.partial(z_landed, step), "pz", lambda copy: copy.wait_recv())
         if step > 0:
             on_faces(functools.partial(x_copy, step - 1), "px", lambda copy: copy.wait_send())
 
-        def arrive(c, step=step):
+        if step == STEPS - 1:
+            break
+
+        def meet(c, step=step):
             for side in (0, 1):
                 @pl.when(has["py"][side])
                 def _():
-                    y_landed(step, side, c).wait_recv()
-                    if step > 0:
-                        y_copy(step - 1, side, c).wait_send()
-
-        def span(low, high, step=step, old=old):
-            @pl.loop(low, high)
-            def _(r):
-                advance(step, r, lambda y: old[y, r - 1], lambda y: old[y, r + 1])
-
-        arrive(0)
-        advance(step, 0, lambda y: hx[0, step, y], lambda y: old[y, 1])
-        span(1, size)
+                    arrive(step, side, c)
+
+        meet(0)
+        head_rows(step, size, every)
 
         @pl.loop(1, chunks - 1)
         def _(c):
-            arrive(c)
-            span(c * size, c * size + size)
-            if step < STEPS - 1:
-                start_y(step + 1, c - 1)
-
-        arrive(chunks - 1)
-        span(rows - size, rows - 1)
-        advance(step, rows - 1, lambda y: old[y, rows - 2], lambda y: hx[1, step, y])
-        if step < STEPS - 1:
-            start_y(step + 1, chunks - 2)
-            on_faces(functools.partial(x_copy, step + 1), "px", lambda copy: copy.start())
-            on_faces(functools.partial(z_copy, step + 1), "pz", lambda copy: copy.start())
-            start_y(step + 1, chunks - 1)
-
-    on_faces(functools.partial(x_copy, STEPS - 1), "px", lambda copy: copy.wait_send())
-    for step in range(STEPS):
-        on_faces(functools.partial(z_copy, step), "pz", lambda copy: copy.wait_send())
+            meet(c)
+            span(step, c * size, c * size + size, every)
+            start_y(step + 1, c - 1)
+
+        meet(chunks - 1)
+        tail_rows(step, rows - size, every)
+        start_y(step + 1, chunks - 2)
+        on_faces(functools.partial(x_copy, step + 1), "px", lambda copy: copy.start())
+        on_faces(functools.partial(z_copy, step + 1), "pz", lambda copy: copy.start())
+        start_y(step + 1, chunks - 1)
+
+    step = STEPS - 1
+    on_faces(functools.partial(x_copy, step), "px", lambda copy: copy.wait_send())
+    for before in range(STEPS):
+        on_faces(functools.partial(z_copy, before), "pz", lambda copy: copy.wait_send())
+
+    def whole(ys):
+        head_rows(step, size, ys)
+        tail_rows(step, size, ys)
+
+    if planes > 2:
+        whole(every[1:-1])
+    for side in (0, 1):
+        @pl.when(jnp.logical_not(has["py"][side]))
+        def _():
+            whole((every[-side],))
+
+    def outer(c, rows_of):
+        for side in (0, 1):
+            @pl.when(has["py"][side])
+            def _():
+                arrive(step, side, c)
+                rows_of((every[-side],))
+
+    outer(0, lambda ys: head_rows(step, size, ys))
+
+    @pl.loop(1, chunks - 1)
+    def _(c):
+        outer(c, lambda ys: span(step, c * size, c * size + size, ys))
+
+    outer(chunks - 1, lambda ys: tail_rows(step, rows - size, ys))
 
     @pl.loop(0, chunks)
     def _(c):
         on_faces(lambda side: y_copy(STEPS - 1, side, c), "py", lambda copy: copy.wait_send())
+
+
+def deliver(parts, held_ref, out_ref, sems):
+    planes, rows = out_ref.shape[:2]
+    size = rows // parts
+    copies = [
+        pltpu.make_async_copy(
+            held_ref.at[y, pl.ds(p * size, size)], out_ref.at[y, pl.ds(p * size, size)], sems.at[y, p])
+        for y in range(planes) for p in range(parts)
+    ]
+    for copy in copies:
+        copy.start()
+    for copy in copies:
+        copy.wait()
 
 
 def local(sizes, initial_density, inverse_limit):
     planes, rows, depth, lanes = initial_density.shape
     chunks = rows // chunk_rows(rows)
     dma = pltpu.SemaphoreType.DMA
-    return pl.pallas_call(
+    held = pl.pallas_call(
         functools.partial(kernel, sizes),
         out_shape=pltpu.VMEM(initial_density.shape, jnp.float32),
         in_specs=[pl.BlockSpec(memory_space=pltpu.HBM)] * 2,
@@ -241,6 +296,16 @@
             collective_id=0, has_side_effects=True, vmem_limit_bytes=50 * 2**20),
         name="populate",
     )(initial_density, inverse_limit)
+    parts = PARTS if rows % PARTS == 0 else 1
+    return pl.pallas_call(
+        functools.partial(deliver, parts),
+        out_shape=jax.ShapeDtypeStruct(initial_density.shape, jnp.float32),
+        in_specs=[pl.BlockSpec(memory_space=pltpu.VMEM)],
+        out_specs=pl.BlockSpec(memory_space=pltpu.HBM),
+        scratch_shapes=[dma((planes, parts))],
+        compiler_params=pltpu.CompilerParams(vmem_limit_bytes=2**20),
+        name="deliver",
+    )(pltpu.with_memory_space_constraint(held, pltpu.VMEM))
 
 
 def solution(mesh):

time: 215 us -> 215 us (level)
  Pallas kernels: 210 us -> 215 us
  local copies, waits for them, and re-layouts: 4.78 us -> 0 us
    unnamed x1 -> x0, local copies, waits for them, and re-layouts: 4.78 us -> none
    pallas_call x0 -> x1, Pallas kernels: none -> 4.7 us  [local(): pl.pallas_call(functools.partial(deliver, parts), out_shape=jax.ShapeDtyp...]
where the time goes in v2:
time: 215 us
  Pallas kernels  215 us (100%)
    pallas_call x1, Pallas kernels, local(): pl.pallas_call(functools.partial(kernel, sizes), out_shape=pltpu.VMEM(ini...  210 us
    pallas_call x1, Pallas kernels, local(): pl.pallas_call(functools.partial(deliver, parts), out_shape=jax.ShapeDtyp...  4.7 us

profile of v2, /device:TPU:0, one launch (start us, length us, event | category | flops | bytes accessed | tf_op | source)
XLA Modules:
  0.0 214.8 jit_solution(1758042532384381933)
XLA Ops:
  0.0 210.1 %populate.1.held_ref = f32[4,64,96,128]{3,2,1,0:T(8,128)S(1)} custom-call(f32[4,64,96,128]{3,2,1,0:T(8,128)} %x_ref.1, f32[4,64,96,128]{3,2,1,0:T(8,128)} %il_ref.1), custom_call_target="tpu_custom_call" | custom-call | tf_op jit(solution)/shard_map/populate/pallas_call | solution.py:279
  210.1 4.7 %deliver.1 = f32[4,64,96,128]{3,2,1,0:T(8,128)} custom-call(f32[4,64,96,128]{3,2,1,0:T(8,128)S(1)} %populate.1.held_ref), custom_call_target="tpu_custom_call" | custom-call | tf_op jit(solution)/shard_map/deliver/pallas_call | solution.py:300
